TPU v7x, 32 devices: a whole 2x2x4 slice. The times are simulated.
32 devices in a mesh: grp: 2 (over y), seq: 4 (over z), head: 2 (over x), rep: 2 (over core).
Axes of the slice: x: 2, y: 2, z: 4, core: 2. Of those that a mesh axis runs over, the one named last changes fastest.
Arguments:
- queries: bfloat16 [16, 4096], P(('grp', 'rep'), 'head'), parts along dimension 0, may hold values from -6 to 6
- k_cache: bfloat16 [16, 16, 4096, 128], P(('grp', 'rep'), 'head', 'seq'), parts along dimension 0, may hold values from -6 to 6
- v_cache: bfloat16 [16, 16, 4096, 128], P(('grp', 'rep'), 'head', 'seq'), parts along dimension 0, may hold values from -6 to 6
- page_table: int32 [16, 32], P(('grp', 'rep')), parts along dimension 0, may hold values from 0 to 31, each once within a row
- lengths: int32 [16], P(('grp', 'rep')), parts along dimension 0, may hold values from 512 to 4096
- keep_threshold: int32 [16, 16], P(('grp', 'rep'), 'head'), parts along dimension 0, may hold values from 256 to 8191
Outputs:
- attended: bfloat16 [16, 4096], P(('grp', 'rep'), 'head'), parts along dimension 0
- token_mass: float32 [16, 16, 4096], P(('grp', 'rep'), 'head', 'seq'), parts along dimension 0
- page_keep: float32 [16, 16, 32], P(('grp', 'rep'), 'head', 'seq'), parts along dimension 0
There are 2 independent parts, one for each index of `grp`. A program takes and returns all parts, laid end to end along the dimension named above; each array names one. Nothing has to cross between parts.
Inputs may be any that keep to these rules, and one draw needn't show every extreme that they name: `page_table`: each row names every physical page slot 0 to 31 once.
All inputs are finite; a program needn't handle non-finite values.
Results may differ from a plain program's by a relative error of at most 0.0052.
Values sent between devices are 32-bit elements; how exact they have to be, the bound alone decides.
No kernel may reach another device: no remote copies, remote signals or barrier semaphores. Data moves between devices by JAX's collectives and lax.ppermute only.
A program may use at most 64 MiB of HBM per device.

v0:
```python
import jax
import jax.numpy as jnp
from jax import lax
from jax.experimental import pallas as pl
from jax.experimental.pallas import tpu as pltpu
from jax.sharding import PartitionSpec as P


PAGE = 128

softcap = 50.0
query_scale = 1.0 / 12.0
quanta = 65536.0


def finish_kernel(table, threshold, *refs):
    ranks = len(refs) - 2
    pieces = refs[:ranks]
    mass, keep = refs[ranks:]
    requests, kv, tok = mass.shape
    pages = tok // PAGE
    seq = lax.axis_index("seq")
    lane = lax.broadcasted_iota(jnp.int32, (kv, pages), 1)
    eye = lax.broadcasted_iota(jnp.int32, (kv, kv), 0) == lax.broadcasted_iota(jnp.int32, (kv, kv), 1)
    for r in range(requests):
        sums = jnp.zeros((kv, pages), jnp.float32)
        for m in range(pages):
            slot = table[r, seq * pages + m]
            away = seq ^ (slot // pages)
            at = pl.multiple_of(slot % pages * PAGE, PAGE)
            page = pieces[0][r, :, pl.ds(at, PAGE)]
            for b in range(1, ranks):
                page = jnp.where(away == b, pieces[b][r, :, pl.ds(at, PAGE)], page)
            mass[r, :, m * PAGE:(m + 1) * PAGE] = page
            sums = jnp.where(lane == m, jnp.sum(page, axis=1, keepdims=True), sums)
        bar = threshold[r:r + 1, :].astype(jnp.float32)
        bar = jnp.sum(jnp.where(eye, bar, 0.0), axis=1, keepdims=True)
        keep[r] = jnp.minimum(1.0, quanta * sums / bar)


def program(ranks):
    assert ranks & (ranks - 1) == 0
    bits = [1 << b for b in reversed(range(ranks.bit_length() - 1))]

    def swap(x, bit):
        return lax.ppermute(x, "seq", [(i, i ^ bit) for i in range(ranks)])

    def direct_sum(x):
        parts = [x] + [swap(x, s) for s in range(1, ranks)]
        while len(parts) > 1:
            half = len(parts) // 2
            parts = [a + b for a, b in zip(parts[:half], parts[half:])]
        return parts[0]

    def staged_sum(x):
        for bit in bits:
            x = x + swap(x, bit)
        return x

    def spread(x):
        parts = {0: x}
        for bit in bits:
            for s, part in list(parts.items()):
                parts[s ^ bit] = swap(part, bit)
        return [parts[s] for s in range(ranks)]

    def shards(queries, k_cache, v_cache, page_table, lengths, keep_threshold):
        requests, kv, tok, hd = k_cache.shape
        heads = queries.shape[1] // hd
        group = heads // kv
        pages = tok // PAGE
        pages_all = page_table.shape[1]
        slot_ids = lax.axis_index("seq") * pages + jnp.arange(pages, dtype=jnp.int32)
        matches = page_table[:, None, :] == slot_ids[None, :, None]
        order = jnp.arange(pages_all, dtype=jnp.int32)[None, None, :]
        logical = jnp.sum(jnp.where(matches, order, 0), axis=2)
        offset = jnp.arange(PAGE, dtype=jnp.int32)[None, None, :]
        position = (logical[:, :, None] * PAGE + offset).reshape(requests, tok)
        is_live = position < lengths[:, None]
        grouped = queries.reshape(requests, kv, group, hd)
        logits = jnp.einsum("rkgd,rktd->rkgt", grouped, k_cache, preferred_element_type=jnp.float32)
        capped = softcap * jnp.tanh(logits * query_scale / softcap)
        weights = jnp.where(is_live[:, None, None, :], jnp.exp(capped - softcap), 0.0)
        denom = direct_sum(jnp.sum(weights, axis=3))
        numer = jnp.einsum(
            "rkgt,rktd->rkgd", weights.astype(jnp.bfloat16), v_cache, preferred_element_type=jnp.float32
        )
        pieces = spread(jnp.sum(weights / denom[..., None], axis=2))
        numer = staged_sum(numer)
        attended = (numer / denom[..., None]).astype(jnp.bfloat16).reshape(requests, heads * hd)
        smem = pl.BlockSpec(memory_space=pltpu.SMEM)
        vmem = pl.BlockSpec(memory_space=pltpu.VMEM)
        mass, keep = pl.pallas_call(
            finish_kernel,
            in_specs=[smem, vmem] + [vmem] * ranks,
            out_specs=[vmem, vmem],
            out_shape=[
                jax.ShapeDtypeStruct((requests, kv, tok), jnp.float32),
                jax.ShapeDtypeStruct((requests, kv, pages), jnp.float32),
            ],
            name="finish",
        )(page_table, keep_threshold, *[pltpu.with_memory_space_constraint(p, pltpu.VMEM) for p in pieces])
        return attended, mass, keep

    return shards


def solution(mesh):
    placed = (
        P(("grp", "rep"), "head"),
        P(("grp", "rep"), "head", "seq", None),
        P(("grp", "rep"), "head", "seq", None),
        P(("grp", "rep"), None),
        P(("grp", "rep")),
        P(("grp", "rep"), "head"),
    )
    ranks = mesh.shape["seq"]
    body = program(ranks)

    return jax.shard_map(
        body,
        mesh=mesh,
        in_specs=placed,
        out_specs=(
            P(("grp", "rep"), "head"),
            P(("grp", "rep"), "head", "seq"),
            P(("grp", "rep"), "head", "seq"),
        ),
        check_vma=False,
    )
```

profile of v0, /device:TPU:0, one launch (start us, length us, event | category | flops | bytes accessed | tf_op | source)
XLA Modules:
  0.0 37.1 jit_solution(8071769743006823663)
XLA Ops:
  0.7 0.9 %select_reduce_fusion = s32[4,8]{1,0:T(4,128)S(1)} fusion(s32[4,32]{1,0:T(4,128)} %table.1, s32[8]{0:T(128)S(1)} %iota_add_fusion), kind=kLoop, calls=%fused_computation.14 | loop fusion | flops 3040 | bytes 672 | tf_op jit(solution)/shard_map/reduce_sum | solution.py:76
  1.6 0.1 broadcast_bitcast_fusion
  1.6 0.7 %reshape.55 = bf16[4,8,2,128]{3,2,1,0:T(2,128)(2,1)S(1)} reshape(bf16[4,2048]{1,0:T(4,128)(2,1)} %param.6) | data formatting | bytes 32768 | tf_op jit(solution)/shard_map/reshape | solution.py:80
  2.4 0.9 %fusion.8 = pred[4,1024]{1,0:T(4,128)(4,1)S(1)} fusion(s32[1,4,8,128]{3,2,1,0:T(8,128)S(1)} %broadcast_bitcast_fusion, s32[4]{0:T(128)} %param.10, s32[1024]{0:T(1024)S(1)} %iota_bitcast_fusion), kind=kLoop, calls=%fused_computation.12 | loop fusion | flops 8192 | bytes 24592 | tf_op jit(solution)/shard_map/lt | solution.py:79
  3.3 5.9 %fusion.9 = (f32[4,8,2]{2,1,0:T(8,128)S(1)}, f32[4,8,2,1024]{3,2,1,0:T(2,128)S(1)}) fusion(bf16[4,8,2,128]{3,2,1,0:T(2,128)(2,1)S(1)} %reshape.55, bf16[4,8,1024,128]{3,2,1,0:T(8,128)(2,1)} %param.7, pred[4,1024]{1,0:T(4,128)(4,1)S(1)} %fusion.8), kind=kOutput, calls=%fused_computation.19 | convolution fusion | flops 17104832 | bytes 8671488 | tf_op jit(solution)/shard_map/rkgd,rktd->rkgt/dot_general | solution.py:81
  9.2 5.1 %collective-permute-start.4 = (f32[4,8,2]{2,1,0:T(8,128)S(1)}, f32[4,8,2]{2,1,0:T(8,128)S(1)}, u32[]{:S(2)}, u32[]{:S(2)}) collective-permute-start(f32[4,8,2]{2,1,0:T(8,128)S(1)} %get-tuple-element.7), channel_id=1, source_target_pairs={{0,12},{4,8},{8,4},{12,0},{1,13},{5,9},{9,5},{13,1},{2,14},{6,10},... | collective-permute-start | bytes 776 | tf_op jit(solution)/shard_map/ppermute | solution.py:46
  14.3 0.6 %collective-permute-start.2 = (f32[4,8,2]{2,1,0:T(8,128)S(1)}, f32[4,8,2]{2,1,0:T(8,128)S(1)}, u32[]{:S(2)}, u32[]{:S(2)}) collective-permute-start(f32[4,8,2]{2,1,0:T(8,128)S(1)} %get-tuple-element.7), channel_id=1, source_target_pairs={{0,8},{4,12},{8,0},{12,4},{1,9},{5,13},{9,1},{13,5},{2,10},{6,14},... | collective-permute-start | bytes 776 | tf_op jit(solution)/shard_map/ppermute | solution.py:46
  14.9 1.1 %collective-permute-done.4 = f32[4,8,2]{2,1,0:T(8,128)S(1)} collective-permute-done((f32[4,8,2]{2,1,0:T(8,128)S(1)}, f32[4,8,2]{2,1,0:T(8,128)S(1)}, u32[]{:S(2)}, u32[]{:S(2)}) %collective-permute-start.4) | collective-permute-done | bytes 288 | tf_op jit(solution)/shard_map/ppermute | solution.py:46
  16.0 2.0 %collective-permute-done.3 = f32[4,8,2]{2,1,0:T(8,128)S(1)} collective-permute-done((f32[4,8,2]{2,1,0:T(8,128)S(1)}, f32[4,8,2]{2,1,0:T(8,128)S(1)}, u32[]{:S(2)}, u32[]{:S(2)}) %collective-permute-start.3) | collective-permute-done | bytes 288 | tf_op jit(solution)/shard_map/ppermute | solution.py:46
  18.0 0.9 %collective-permute-done.2 = f32[4,8,2]{2,1,0:T(8,128)S(1)} collective-permute-done((f32[4,8,2]{2,1,0:T(8,128)S(1)}, f32[4,8,2]{2,1,0:T(8,128)S(1)}, u32[]{:S(2)}, u32[]{:S(2)}) %collective-permute-start.2) | collective-permute-done | bytes 288 | tf_op jit(solution)/shard_map/ppermute | solution.py:46
  18.9 0.4 %divide_reduce_fusion.refs_0_ = f32[4,8,1024]{2,1,0:T(8,128)S(1)} fusion(f32[4,8,2,1024]{3,2,1,0:T(2,128)S(1)} %get-tuple-element.8, f32[4,8,2]{2,1,0:T(8,128)S(1)} %add_add_fusion), kind=kLoop, calls=%fused_computation.6 | loop fusion | flops 98304 | bytes 393472 | tf_op jit(solution)/shard_map/reduce_sum | solution.py:88
  19.3 0.8 %collective-permute-start.6 = (f32[4,8,1024]{2,1,0:T(8,128)S(1)}, f32[4,8,1024]{2,1,0:T(8,128)S(1)}, u32[]{:S(2)}, u32[]{:S(2)}) collective-permute-start(f32[4,8,1024]{2,1,0:T(8,128)S(1)} %divide_reduce_fusion.refs_0_), channel_id=1, source_target_pairs={{0,8},{4,12},{8,0},{12,4},{1,9},{5,13},{9,1},{13,5},{2,10},{6,14},... | collective-permute-start | bytes 393224 | tf_op jit(solution)/shard_map/ppermute | solution.py:46
  20.1 1.2 %fusion.5 = f32[4,8,2,128]{3,2,1,0:T(2,128)S(1)} fusion(bf16[4,8,1024,128]{3,2,1,0:T(8,128)(2,1)S(1)} %copy-done, f32[4,8,2,1024]{3,2,1,0:T(2,128)S(1)} %get-tuple-element.8), kind=kOutput, calls=%fused_computation.7 | convolution fusion | flops 16842752 | bytes 8683520 | tf_op jit(solution)/shard_map/rkgt,rktd->rkgd/dot_general | solution.py:85
  21.3 2.2 %collective-permute-start = (f32[4,8,2,128]{3,2,1,0:T(2,128)S(1)}, f32[4,8,2,128]{3,2,1,0:T(2,128)S(1)}, u32[]{:S(2)}, u32[]{:S(2)}) collective-permute-start(f32[4,8,2,128]{3,2,1,0:T(2,128)S(1)} %fusion.5), channel_id=1, source_target_pairs={{0,8},{4,12},{8,0},{12,4},{1,9},{5,13},{9,1},{13,5},{2,10},{6,14},... | collective-permute-start | bytes 98312 | tf_op jit(solution)/shard_map/ppermute | solution.py:46
  23.6 4.8 %collective-permute-done = f32[4,8,2,128]{3,2,1,0:T(2,128)S(1)} collective-permute-done((f32[4,8,2,128]{3,2,1,0:T(2,128)S(1)}, f32[4,8,2,128]{3,2,1,0:T(2,128)S(1)}, u32[]{:S(2)}, u32[]{:S(2)}) %collective-permute-start) | collective-permute-done | bytes 32800 | tf_op jit(solution)/shard_map/ppermute | solution.py:46
  28.4 0.1 collective-permute-start.1
  28.4 2.0 %collective-permute-start.5 = (f32[4,8,1024]{2,1,0:T(8,128)S(1)}, f32[4,8,1024]{2,1,0:T(8,128)S(1)}, u32[]{:S(2)}, u32[]{:S(2)}) collective-permute-start(f32[4,8,1024]{2,1,0:T(8,128)S(1)} %divide_reduce_fusion.refs_0_), channel_id=1, source_target_pairs={{0,4},{4,0},{8,12},{12,8},{1,5},{5,1},{9,13},{13,9},{2,6},{6,2},{1... | collective-permute-start | bytes 393224 | tf_op jit(solution)/shard_map/ppermute | solution.py:46
  30.4 0.1 collective-permute-start.7
  30.5 1.8 %collective-permute-done.1 = f32[4,8,2,128]{3,2,1,0:T(2,128)S(1)} collective-permute-done((f32[4,8,2,128]{3,2,1,0:T(2,128)S(1)}, f32[4,8,2,128]{3,2,1,0:T(2,128)S(1)}, u32[]{:S(2)}, u32[]{:S(2)}) %collective-permute-start.1) | collective-permute-done | bytes 32800 | tf_op jit(solution)/shard_map/ppermute | solution.py:46
  32.3 0.1 fusion.7
  32.4 0.6 %reshape.56 = bf16[4,2048]{1,0:T(4,128)(2,1)} reshape(bf16[4,8,2,128]{3,2,1,0:T(2,128)(2,1)S(1)} %fusion.7) | data formatting | bytes 32768 | tf_op jit(solution)/shard_map/reshape | solution.py:90
  33.1 0.7 %collective-permute-done.5.refs_1_ = f32[4,8,1024]{2,1,0:T(8,128)S(1)} collective-permute-done((f32[4,8,1024]{2,1,0:T(8,128)S(1)}, f32[4,8,1024]{2,1,0:T(8,128)S(1)}, u32[]{:S(2)}, u32[]{:S(2)}) %collective-permute-start.5) | collective-permute-done | bytes 131104 | tf_op jit(solution)/shard_map/ppermute | solution.py:46
  33.7 1.7 %collective-permute-done.7.refs_3_ = f32[4,8,1024]{2,1,0:T(8,128)S(1)} collective-permute-done((f32[4,8,1024]{2,1,0:T(8,128)S(1)}, f32[4,8,1024]{2,1,0:T(8,128)S(1)}, u32[]{:S(2)}, u32[]{:S(2)}) %collective-permute-start.7) | collective-permute-done | bytes 131104 | tf_op jit(solution)/shard_map/ppermute | solution.py:46
  35.4 1.7 %finish.1 = (f32[4,8,1024]{2,1,0:T(8,128)}, f32[4,8,8]{2,1,0:T(8,128)}) custom-call(s32[4,32]{1,0:T(4,128)} %table.1, s32[4,8]{1,0:T(4,128)} %threshold.1, f32[4,8,1024]{2,1,0:T(8,128)S(1)} %divide_reduce_fusion.refs_0_, f32[4,8,1024]{2,1,0:T(8,128)S(1)} %collective-permute-done.5.refs_1_, f32[4,8,1024]{2,1,0:T(8,128)S(1)} %collective-permute-done.6.refs_2_, ...), custom_call_target="tpu_custom_call" | custom-call | tf_op jit(solution)/shard_map/finish/pallas_call | solution.py:93
  (9 shorter events, 0.0 us)
Async XLA Ops:
  2.4 17.7 %copy-start = (bf16[4,8,1024,128]{3,2,1,0:T(8,128)(2,1)S(1)}, bf16[4,8,1024,128]{3,2,1,0:T(8,128)(2,1)}, u32[]{:S(2)}) copy-start(bf16[4,8,1024,128]{3,2,1,0:T(8,128)(2,1)} %param.8) | copy-start | bytes 25165828
  9.2 6.8 %collective-permute-start.4 = (f32[4,8,2]{2,1,0:T(8,128)S(1)}, f32[4,8,2]{2,1,0:T(8,128)S(1)}, u32[]{:S(2)}, u32[]{:S(2)}) collective-permute-start(f32[4,8,2]{2,1,0:T(8,128)S(1)} %get-tuple-element.7), channel_id=1, source_target_pairs={{0,12},{4,8},{8,4},{12,0},{1,13},{5,9},{9,5},{13,1},{2,14},{6,10},... | collective-permute-start | bytes 776 | tf_op jit(solution)/shard_map/ppermute | solution.py:46
  14.3 3.7 %collective-permute-start.3 = (f32[4,8,2]{2,1,0:T(8,128)S(1)}, f32[4,8,2]{2,1,0:T(8,128)S(1)}, u32[]{:S(2)}, u32[]{:S(2)}) collective-permute-start(f32[4,8,2]{2,1,0:T(8,128)S(1)} %get-tuple-element.7), channel_id=1, source_target_pairs={{0,4},{4,0},{8,12},{12,8},{1,5},{5,1},{9,13},{13,9},{2,6},{6,2},{1... | collective-permute-start | bytes 776 | tf_op jit(solution)/shard_map/ppermute | solution.py:46
  14.3 4.6 %collective-permute-start.2 = (f32[4,8,2]{2,1,0:T(8,128)S(1)}, f32[4,8,2]{2,1,0:T(8,128)S(1)}, u32[]{:S(2)}, u32[]{:S(2)}) collective-permute-start(f32[4,8,2]{2,1,0:T(8,128)S(1)} %get-tuple-element.7), channel_id=1, source_target_pairs={{0,8},{4,12},{8,0},{12,4},{1,9},{5,13},{9,1},{13,5},{2,10},{6,14},... | collective-permute-start | bytes 776 | tf_op jit(solution)/shard_map/ppermute | solution.py:46
  19.3 11.1 %collective-permute-start.6 = (f32[4,8,1024]{2,1,0:T(8,128)S(1)}, f32[4,8,1024]{2,1,0:T(8,128)S(1)}, u32[]{:S(2)}, u32[]{:S(2)}) collective-permute-start(f32[4,8,1024]{2,1,0:T(8,128)S(1)} %divide_reduce_fusion.refs_0_), channel_id=1, source_target_pairs={{0,8},{4,12},{8,0},{12,4},{1,9},{5,13},{9,1},{13,5},{2,10},{6,14},... | collective-permute-start | bytes 393224 | tf_op jit(solution)/shard_map/ppermute | solution.py:46
  21.3 7.0 %collective-permute-start = (f32[4,8,2,128]{3,2,1,0:T(2,128)S(1)}, f32[4,8,2,128]{3,2,1,0:T(2,128)S(1)}, u32[]{:S(2)}, u32[]{:S(2)}) collective-permute-start(f32[4,8,2,128]{3,2,1,0:T(2,128)S(1)} %fusion.5), channel_id=1, source_target_pairs={{0,8},{4,12},{8,0},{12,4},{1,9},{5,13},{9,1},{13,5},{2,10},{6,14},... | collective-permute-start | bytes 98312 | tf_op jit(solution)/shard_map/ppermute | solution.py:46
  28.4 4.0 %collective-permute-start.1 = (f32[4,8,2,128]{3,2,1,0:T(2,128)S(1)}, f32[4,8,2,128]{3,2,1,0:T(2,128)S(1)}, u32[]{:S(2)}, u32[]{:S(2)}) collective-permute-start(f32[4,8,2,128]{3,2,1,0:T(2,128)S(1)} %add.58), channel_id=1, source_target_pairs={{0,4},{4,0},{8,12},{12,8},{1,5},{5,1},{9,13},{13,9},{2,6},{6,2},{1... | collective-permute-start | bytes 98312 | tf_op jit(solution)/shard_map/ppermute | solution.py:46
  28.4 5.3 %collective-permute-start.5 = (f32[4,8,1024]{2,1,0:T(8,128)S(1)}, f32[4,8,1024]{2,1,0:T(8,128)S(1)}, u32[]{:S(2)}, u32[]{:S(2)}) collective-permute-start(f32[4,8,1024]{2,1,0:T(8,128)S(1)} %divide_reduce_fusion.refs_0_), channel_id=1, source_target_pairs={{0,4},{4,0},{8,12},{12,8},{1,5},{5,1},{9,13},{13,9},{2,6},{6,2},{1... | collective-permute-start | bytes 393224 | tf_op jit(solution)/shard_map/ppermute | solution.py:46
  30.4 5.0 %collective-permute-start.7 = (f32[4,8,1024]{2,1,0:T(8,128)S(1)}, f32[4,8,1024]{2,1,0:T(8,128)S(1)}, u32[]{:S(2)}, u32[]{:S(2)}) collective-permute-start(f32[4,8,1024]{2,1,0:T(8,128)S(1)} %collective-permute-done.6.refs_2_), channel_id=1, source_target_pairs={{0,4},{4,0},{8,12},{12,8},{1,5},{5,1},{9,13},{13,9},{2,6},{6,2},{1... | collective-permute-start | bytes 393224 | tf_op jit(solution)/shard_map/ppermute | solution.py:46
where the time goes:
time: 37.4 us; the launch traced here: 37.1 us
  waiting for transfers between devices  12.9 us (34%)
  starting transfers between devices  10.9 us (29%)
  matrix products  7.08 us (19%)
  other arithmetic  2.33 us (6%)
  Pallas kernels  1.72 us (5%)
  local copies, waits for them, and re-layouts  1.44 us (4%)
  between operations  0.71 us (2%)
    ppermute x8, waiting for transfers between devices, swap(): return lax.ppermute(x, 'seq', [(i, i ^ bit) for i in range(ranks)])  12.9 us
    ppermute x8, starting transfers between devices, swap(): return lax.ppermute(x, 'seq', [(i, i ^ bit) for i in range(ranks)])  10.9 us
    dot_general x1, matrix products, shards(): jnp.einsum('rkgd,rktd->rkgt', grouped, k_cache, preferred_element_type=jn...  5.9 us
    pallas_call x1, Pallas kernels, shards(): pl.pallas_call(finish_kernel, in_specs=[smem, vmem] + [vmem] * ranks, out...  1.72 us
    dot_general x1, matrix products, shards(): jnp.einsum('rkgt,rktd->rkgd', weights.astype(jnp.bfloat16), v_cache, pref...  1.19 us
    reduce_sum x1, other arithmetic, shards(): logical = jnp.sum(jnp.where(matches, order, 0), axis=2)  0.89 us
    lt x1, other arithmetic, shards(): is_live = position < lengths[:, None]  0.88 us
  transfers between devices with their start and end apart: 8, of which 7 were waited for; matrix products, arithmetic and copies ran while one was open for 5% of the time, Pallas kernels for 0%

commit v1 on v0

--- a/solution.py
+++ b/solution.py
@@ -71,9 +71,9 @@
         pages = tok // PAGE
         pages_all = page_table.shape[1]
         slot_ids = lax.axis_index("seq") * pages + jnp.arange(pages, dtype=jnp.int32)
-        matches = page_table[:, None, :] == slot_ids[None, :, None]
-        order = jnp.arange(pages_all, dtype=jnp.int32)[None, None, :]
-        logical = jnp.sum(jnp.where(matches, order, 0), axis=2)
+        matches = page_table[:, :, None] == slot_ids[None, None, :]
+        order = jnp.arange(pages_all, dtype=jnp.int32)[None, :, None]
+        logical = jnp.sum(jnp.where(matches, order, 0), axis=1)
         offset = jnp.arange(PAGE, dtype=jnp.int32)[None, None, :]
         position = (logical[:, :, None] * PAGE + offset).reshape(requests, tok)
         is_live = position < lengths[:, None]

time: 37.4 us -> 37.4 us (level)
  no operation moved by 1% of the time
where the time goes in v1:
time: 37.4 us; the launch traced here: 37.1 us
  waiting for transfers between devices  12.9 us (34%)
  starting transfers between devices  10.9 us (29%)
  matrix products  7.08 us (19%)
  other arithmetic  2.33 us (6%)
  Pallas kernels  1.72 us (5%)
  local copies, waits for them, and re-layouts  1.44 us (4%)
  between operations  0.71 us (2%)
    ppermute x8, waiting for transfers between devices, swap(): return lax.ppermute(x, 'seq', [(i, i ^ bit) for i in range(ranks)])  12.9 us
    ppermute x8, starting transfers between devices, swap(): return lax.ppermute(x, 'seq', [(i, i ^ bit) for i in range(ranks)])  10.9 us
    dot_general x1, matrix products, shards(): jnp.einsum('rkgd,rktd->rkgt', grouped, k_cache, preferred_element_type=jn...  5.9 us
    pallas_call x1, Pallas kernels, shards(): pl.pallas_call(finish_kernel, in_specs=[smem, vmem] + [vmem] * ranks, out...  1.72 us
    dot_general x1, matrix products, shards(): jnp.einsum('rkgt,rktd->rkgd', weights.astype(jnp.bfloat16), v_cache, pref...  1.19 us
    reduce_sum x1, other arithmetic, shards(): logical = jnp.sum(jnp.where(matches, order, 0), axis=1)  0.89 us
    lt x1, other arithmetic, shards(): is_live = position < lengths[:, None]  0.88 us
  transfers between devices with their start and end apart: 8, of which 7 were waited for; matrix products, arithmetic and copies ran while one was open for 5% of the time, Pallas kernels for 0%

profile of v1, /device:TPU:0, one launch (start us, length us, event | category | flops | bytes accessed | tf_op | source)
XLA Modules:
  0.0 37.1 jit_solution(8071769743006823663)
XLA Ops:
  0.7 0.9 %select_reduce_fusion = s32[4,8]{1,0:T(4,128)S(1)} fusion(s32[4,32]{1,0:T(4,128)} %table.1, s32[8]{0:T(128)S(1)} %iota_add_fusion), kind=kLoop, calls=%fused_computation.14 | loop fusion | flops 3040 | bytes 672 | tf_op jit(solution)/shard_map/reduce_sum | solution.py:76
  1.6 0.1 broadcast_bitcast_fusion
  1.6 0.7 %reshape.55 = bf16[4,8,2,128]{3,2,1,0:T(2,128)(2,1)S(1)} reshape(bf16[4,2048]{1,0:T(4,128)(2,1)} %param.6) | data formatting | bytes 32768 | tf_op jit(solution)/shard_map/reshape | solution.py:80
  2.4 0.9 %fusion.8 = pred[4,1024]{1,0:T(4,128)(4,1)S(1)} fusion(s32[1,4,8,128]{3,2,1,0:T(8,128)S(1)} %broadcast_bitcast_fusion, s32[4]{0:T(128)} %param.10, s32[1024]{0:T(1024)S(1)} %iota_bitcast_fusion), kind=kLoop, calls=%fused_computation.12 | loop fusion | flops 8192 | bytes 24592 | tf_op jit(solution)/shard_map/lt | solution.py:79
  3.3 5.9 %fusion.9 = (f32[4,8,2]{2,1,0:T(8,128)S(1)}, f32[4,8,2,1024]{3,2,1,0:T(2,128)S(1)}) fusion(bf16[4,8,2,128]{3,2,1,0:T(2,128)(2,1)S(1)} %reshape.55, bf16[4,8,1024,128]{3,2,1,0:T(8,128)(2,1)} %param.7, pred[4,1024]{1,0:T(4,128)(4,1)S(1)} %fusion.8), kind=kOutput, calls=%fused_computation.19 | convolution fusion | flops 17104832 | bytes 8671488 | tf_op jit(solution)/shard_map/rkgd,rktd->rkgt/dot_general | solution.py:81
  9.2 5.1 %collective-permute-start.4 = (f32[4,8,2]{2,1,0:T(8,128)S(1)}, f32[4,8,2]{2,1,0:T(8,128)S(1)}, u32[]{:S(2)}, u32[]{:S(2)}) collective-permute-start(f32[4,8,2]{2,1,0:T(8,128)S(1)} %get-tuple-element.7), channel_id=1, source_target_pairs={{0,12},{4,8},{8,4},{12,0},{1,13},{5,9},{9,5},{13,1},{2,14},{6,10},... | collective-permute-start | bytes 776 | tf_op jit(solution)/shard_map/ppermute | solution.py:46
  14.3 0.6 %collective-permute-start.2 = (f32[4,8,2]{2,1,0:T(8,128)S(1)}, f32[4,8,2]{2,1,0:T(8,128)S(1)}, u32[]{:S(2)}, u32[]{:S(2)}) collective-permute-start(f32[4,8,2]{2,1,0:T(8,128)S(1)} %get-tuple-element.7), channel_id=1, source_target_pairs={{0,8},{4,12},{8,0},{12,4},{1,9},{5,13},{9,1},{13,5},{2,10},{6,14},... | collective-permute-start | bytes 776 | tf_op jit(solution)/shard_map/ppermute | solution.py:46
  14.9 1.1 %collective-permute-done.4 = f32[4,8,2]{2,1,0:T(8,128)S(1)} collective-permute-done((f32[4,8,2]{2,1,0:T(8,128)S(1)}, f32[4,8,2]{2,1,0:T(8,128)S(1)}, u32[]{:S(2)}, u32[]{:S(2)}) %collective-permute-start.4) | collective-permute-done | bytes 288 | tf_op jit(solution)/shard_map/ppermute | solution.py:46
  16.0 2.0 %collective-permute-done.3 = f32[4,8,2]{2,1,0:T(8,128)S(1)} collective-permute-done((f32[4,8,2]{2,1,0:T(8,128)S(1)}, f32[4,8,2]{2,1,0:T(8,128)S(1)}, u32[]{:S(2)}, u32[]{:S(2)}) %collective-permute-start.3) | collective-permute-done | bytes 288 | tf_op jit(solution)/shard_map/ppermute | solution.py:46
  18.0 0.9 %collective-permute-done.2 = f32[4,8,2]{2,1,0:T(8,128)S(1)} collective-permute-done((f32[4,8,2]{2,1,0:T(8,128)S(1)}, f32[4,8,2]{2,1,0:T(8,128)S(1)}, u32[]{:S(2)}, u32[]{:S(2)}) %collective-permute-start.2) | collective-permute-done | bytes 288 | tf_op jit(solution)/shard_map/ppermute | solution.py:46
  18.9 0.4 %divide_reduce_fusion.refs_0_ = f32[4,8,1024]{2,1,0:T(8,128)S(1)} fusion(f32[4,8,2,1024]{3,2,1,0:T(2,128)S(1)} %get-tuple-element.8, f32[4,8,2]{2,1,0:T(8,128)S(1)} %add_add_fusion), kind=kLoop, calls=%fused_computation.6 | loop fusion | flops 98304 | bytes 393472 | tf_op jit(solution)/shard_map/reduce_sum | solution.py:88
  19.3 0.8 %collective-permute-start.6 = (f32[4,8,1024]{2,1,0:T(8,128)S(1)}, f32[4,8,1024]{2,1,0:T(8,128)S(1)}, u32[]{:S(2)}, u32[]{:S(2)}) collective-permute-start(f32[4,8,1024]{2,1,0:T(8,128)S(1)} %divide_reduce_fusion.refs_0_), channel_id=1, source_target_pairs={{0,8},{4,12},{8,0},{12,4},{1,9},{5,13},{9,1},{13,5},{2,10},{6,14},... | collective-permute-start | bytes 393224 | tf_op jit(solution)/shard_map/ppermute | solution.py:46
  20.1 1.2 %fusion.5 = f32[4,8,2,128]{3,2,1,0:T(2,128)S(1)} fusion(bf16[4,8,1024,128]{3,2,1,0:T(8,128)(2,1)S(1)} %copy-done, f32[4,8,2,1024]{3,2,1,0:T(2,128)S(1)} %get-tuple-element.8), kind=kOutput, calls=%fused_computation.7 | convolution fusion | flops 16842752 | bytes 8683520 | tf_op jit(solution)/shard_map/rkgt,rktd->rkgd/dot_general | solution.py:85
  21.3 2.2 %collective-permute-start = (f32[4,8,2,128]{3,2,1,0:T(2,128)S(1)}, f32[4,8,2,128]{3,2,1,0:T(2,128)S(1)}, u32[]{:S(2)}, u32[]{:S(2)}) collective-permute-start(f32[4,8,2,128]{3,2,1,0:T(2,128)S(1)} %fusion.5), channel_id=1, source_target_pairs={{0,8},{4,12},{8,0},{12,4},{1,9},{5,13},{9,1},{13,5},{2,10},{6,14},... | collective-permute-start | bytes 98312 | tf_op jit(solution)/shard_map/ppermute | solution.py:46
  23.6 4.8 %collective-permute-done = f32[4,8,2,128]{3,2,1,0:T(2,128)S(1)} collective-permute-done((f32[4,8,2,128]{3,2,1,0:T(2,128)S(1)}, f32[4,8,2,128]{3,2,1,0:T(2,128)S(1)}, u32[]{:S(2)}, u32[]{:S(2)}) %collective-permute-start) | collective-permute-done | bytes 32800 | tf_op jit(solution)/shard_map/ppermute | solution.py:46
  28.4 0.1 collective-permute-start.1
  28.4 2.0 %collective-permute-start.5 = (f32[4,8,1024]{2,1,0:T(8,128)S(1)}, f32[4,8,1024]{2,1,0:T(8,128)S(1)}, u32[]{:S(2)}, u32[]{:S(2)}) collective-permute-start(f32[4,8,1024]{2,1,0:T(8,128)S(1)} %divide_reduce_fusion.refs_0_), channel_id=1, source_target_pairs={{0,4},{4,0},{8,12},{12,8},{1,5},{5,1},{9,13},{13,9},{2,6},{6,2},{1... | collective-permute-start | bytes 393224 | tf_op jit(solution)/shard_map/ppermute | solution.py:46
  30.4 0.1 collective-permute-start.7
  30.5 1.8 %collective-permute-done.1 = f32[4,8,2,128]{3,2,1,0:T(2,128)S(1)} collective-permute-done((f32[4,8,2,128]{3,2,1,0:T(2,128)S(1)}, f32[4,8,2,128]{3,2,1,0:T(2,128)S(1)}, u32[]{:S(2)}, u32[]{:S(2)}) %collective-permute-start.1) | collective-permute-done | bytes 32800 | tf_op jit(solution)/shard_map/ppermute | solution.py:46
  32.3 0.1 fusion.7
  32.4 0.6 %reshape.56 = bf16[4,2048]{1,0:T(4,128)(2,1)} reshape(bf16[4,8,2,128]{3,2,1,0:T(2,128)(2,1)S(1)} %fusion.7) | data formatting | bytes 32768 | tf_op jit(solution)/shard_map/reshape | solution.py:90
  33.1 0.7 %collective-permute-done.5.refs_1_ = f32[4,8,1024]{2,1,0:T(8,128)S(1)} collective-permute-done((f32[4,8,1024]{2,1,0:T(8,128)S(1)}, f32[4,8,1024]{2,1,0:T(8,128)S(1)}, u32[]{:S(2)}, u32[]{:S(2)}) %collective-permute-start.5) | collective-permute-done | bytes 131104 | tf_op jit(solution)/shard_map/ppermute | solution.py:46
  33.7 1.7 %collective-permute-done.7.refs_3_ = f32[4,8,1024]{2,1,0:T(8,128)S(1)} collective-permute-done((f32[4,8,1024]{2,1,0:T(8,128)S(1)}, f32[4,8,1024]{2,1,0:T(8,128)S(1)}, u32[]{:S(2)}, u32[]{:S(2)}) %collective-permute-start.7) | collective-permute-done | bytes 131104 | tf_op jit(solution)/shard_map/ppermute | solution.py:46
  35.4 1.7 %finish.1 = (f32[4,8,1024]{2,1,0:T(8,128)}, f32[4,8,8]{2,1,0:T(8,128)}) custom-call(s32[4,32]{1,0:T(4,128)} %table.1, s32[4,8]{1,0:T(4,128)} %threshold.1, f32[4,8,1024]{2,1,0:T(8,128)S(1)} %divide_reduce_fusion.refs_0_, f32[4,8,1024]{2,1,0:T(8,128)S(1)} %collective-permute-done.5.refs_1_, f32[4,8,1024]{2,1,0:T(8,128)S(1)} %collective-permute-done.6.refs_2_, ...), custom_call_target="tpu_custom_call" | custom-call | tf_op jit(solution)/shard_map/finish/pallas_call | solution.py:93
  (9 shorter events, 0.0 us)
Async XLA Ops:
  2.4 17.7 %copy-start = (bf16[4,8,1024,128]{3,2,1,0:T(8,128)(2,1)S(1)}, bf16[4,8,1024,128]{3,2,1,0:T(8,128)(2,1)}, u32[]{:S(2)}) copy-start(bf16[4,8,1024,128]{3,2,1,0:T(8,128)(2,1)} %param.8) | copy-start | bytes 25165828
  9.2 6.8 %collective-permute-start.4 = (f32[4,8,2]{2,1,0:T(8,128)S(1)}, f32[4,8,2]{2,1,0:T(8,128)S(1)}, u32[]{:S(2)}, u32[]{:S(2)}) collective-permute-start(f32[4,8,2]{2,1,0:T(8,128)S(1)} %get-tuple-element.7), channel_id=1, source_target_pairs={{0,12},{4,8},{8,4},{12,0},{1,13},{5,9},{9,5},{13,1},{2,14},{6,10},... | collective-permute-start | bytes 776 | tf_op jit(solution)/shard_map/ppermute | solution.py:46
  14.3 3.7 %collective-permute-start.3 = (f32[4,8,2]{2,1,0:T(8,128)S(1)}, f32[4,8,2]{2,1,0:T(8,128)S(1)}, u32[]{:S(2)}, u32[]{:S(2)}) collective-permute-start(f32[4,8,2]{2,1,0:T(8,128)S(1)} %get-tuple-element.7), channel_id=1, source_target_pairs={{0,4},{4,0},{8,12},{12,8},{1,5},{5,1},{9,13},{13,9},{2,6},{6,2},{1... | collective-permute-start | bytes 776 | tf_op jit(solution)/shard_map/ppermute | solution.py:46
  14.3 4.6 %collective-permute-start.2 = (f32[4,8,2]{2,1,0:T(8,128)S(1)}, f32[4,8,2]{2,1,0:T(8,128)S(1)}, u32[]{:S(2)}, u32[]{:S(2)}) collective-permute-start(f32[4,8,2]{2,1,0:T(8,128)S(1)} %get-tuple-element.7), channel_id=1, source_target_pairs={{0,8},{4,12},{8,0},{12,4},{1,9},{5,13},{9,1},{13,5},{2,10},{6,14},... | collective-permute-start | bytes 776 | tf_op jit(solution)/shard_map/ppermute | solution.py:46
  19.3 11.1 %collective-permute-start.6 = (f32[4,8,1024]{2,1,0:T(8,128)S(1)}, f32[4,8,1024]{2,1,0:T(8,128)S(1)}, u32[]{:S(2)}, u32[]{:S(2)}) collective-permute-start(f32[4,8,1024]{2,1,0:T(8,128)S(1)} %divide_reduce_fusion.refs_0_), channel_id=1, source_target_pairs={{0,8},{4,12},{8,0},{12,4},{1,9},{5,13},{9,1},{13,5},{2,10},{6,14},... | collective-permute-start | bytes 393224 | tf_op jit(solution)/shard_map/ppermute | solution.py:46
  21.3 7.0 %collective-permute-start = (f32[4,8,2,128]{3,2,1,0:T(2,128)S(1)}, f32[4,8,2,128]{3,2,1,0:T(2,128)S(1)}, u32[]{:S(2)}, u32[]{:S(2)}) collective-permute-start(f32[4,8,2,128]{3,2,1,0:T(2,128)S(1)} %fusion.5), channel_id=1, source_target_pairs={{0,8},{4,12},{8,0},{12,4},{1,9},{5,13},{9,1},{13,5},{2,10},{6,14},... | collective-permute-start | bytes 98312 | tf_op jit(solution)/shard_map/ppermute | solution.py:46
  28.4 4.0 %collective-permute-start.1 = (f32[4,8,2,128]{3,2,1,0:T(2,128)S(1)}, f32[4,8,2,128]{3,2,1,0:T(2,128)S(1)}, u32[]{:S(2)}, u32[]{:S(2)}) collective-permute-start(f32[4,8,2,128]{3,2,1,0:T(2,128)S(1)} %add.58), channel_id=1, source_target_pairs={{0,4},{4,0},{8,12},{12,8},{1,5},{5,1},{9,13},{13,9},{2,6},{6,2},{1... | collective-permute-start | bytes 98312 | tf_op jit(solution)/shard_map/ppermute | solution.py:46
  28.4 5.3 %collective-permute-start.5 = (f32[4,8,1024]{2,1,0:T(8,128)S(1)}, f32[4,8,1024]{2,1,0:T(8,128)S(1)}, u32[]{:S(2)}, u32[]{:S(2)}) collective-permute-start(f32[4,8,1024]{2,1,0:T(8,128)S(1)} %divide_reduce_fusion.refs_0_), channel_id=1, source_target_pairs={{0,4},{4,0},{8,12},{12,8},{1,5},{5,1},{9,13},{13,9},{2,6},{6,2},{1... | collective-permute-start | bytes 393224 | tf_op jit(solution)/shard_map/ppermute | solution.py:46
  30.4 5.0 %collective-permute-start.7 = (f32[4,8,1024]{2,1,0:T(8,128)S(1)}, f32[4,8,1024]{2,1,0:T(8,128)S(1)}, u32[]{:S(2)}, u32[]{:S(2)}) collective-permute-start(f32[4,8,1024]{2,1,0:T(8,128)S(1)} %collective-permute-done.6.refs_2_), channel_id=1, source_target_pairs={{0,4},{4,0},{8,12},{12,8},{1,5},{5,1},{9,13},{13,9},{2,6},{6,2},{1... | collective-permute-start | bytes 393224 | tf_op jit(solution)/shard_map/ppermute | solution.py:46
